TPU v7x, 32 devices: a whole 2x2x4 slice. The times are simulated.
32 devices in a mesh: dev: 32 (over z, y, x, core).
Axes of the slice: x: 2, y: 2, z: 4, core: 2. Of those that a mesh axis runs over, the one named last changes fastest.
Arguments:
- pixels: float32 [4, 512, 8192], P(None, 'dev'), may hold values from -10 to 10
- valid_flags: int32 [4, 512, 8192], P(None, 'dev'), may hold values 0 or 1
Outputs:
- tile_halves: float32 [32, 256, 2048], P('dev')
- header: float32 [5, 4], replicated
All inputs are finite; a program needn't handle non-finite values. No bound on the sum of `valid_flags` on one device may be relied on, other than what follows from the above.
Results may differ from a plain program's by a relative error of at most 0.00002.
Values sent between devices are 32-bit elements; how exact they have to be, the bound alone decides.
A program may use at most 128 MiB of HBM per device.

v0:
```python
import functools

import jax
import jax.numpy as jnp
from jax import lax
from jax.experimental import pallas as pl
from jax.experimental.pallas import tpu as pltpu
from jax.sharding import PartitionSpec as P

TILE = 512
LANES = 128
SUBLANES = 8
STATS = 5
SLOT = 8
WINDOW = 3
EARLY = 2

largest_value = 3e38


def partner_of(position, mask, bits):
    partner = position
    for bit in range(bits):
        own = position // (1 << bit) % 2
        flip = mask // (1 << bit) % 2
        partner = partner + flip * (1 - 2 * own) * (1 << bit)
    return partner


def schedule(members):
    whole = members // 2 - 1
    pairs = sorted((min(high, whole - high, key=lambda h: (-h.bit_count(), h))
                    for high in range(1, whole // 2 + 1)))
    groups = [[(whole, 1)], [(whole, 0)]]
    groups += [[(a, core), (whole - a, core)] for a in pairs for core in (0, 1)]
    groups.append([(0, 1)])
    masks, slots = [], []
    for group in groups:
        slots.append(range(len(masks), len(masks) + len(group)))
        masks += [high * 2 + core for high, core in group]
    return masks + [0], slots


def lane_tables(bands):
    block = LANES // bands
    lane = lax.broadcasted_iota(jnp.int32, (SUBLANES, LANES), 1)
    m, r = lane // bands, lane % bands
    spread = [(r - b + bands) % bands * block + m for b in range(bands)]
    fix = [m * bands + (r + j) % bands for j in range(bands)]
    return r, spread, fix


def permute(x, index):
    return jnp.take_along_axis(x, index, axis=1, mode="promise_in_bounds")


def merge_rows(stats):
    which = lax.broadcasted_iota(jnp.int32, (1, LANES), 1) % SLOT
    low = jnp.min(stats, axis=0, keepdims=True)
    high = jnp.max(stats, axis=0, keepdims=True)
    total = jnp.sum(stats, axis=0, keepdims=True)
    return jnp.where(which == 0, low, jnp.where(which == 1, high, total))


def exchange(n, members, early, pix_ref, flag_ref, out_ref, stat_out, pix, flag, send, row, rows_in,
             load_sem, send_sem, recv_sem, row_send, row_recv):
    bands, rows, _ = pix_ref.shape
    bits = members.bit_length() - 1
    me = lax.axis_index("dev")
    position = me % members
    first = me - position

    barrier = pltpu.get_barrier_semaphore()

    groups = n // members

    def mate(k):
        return first + (position + k) % members

    def twin(k):
        return (me + k * members) % n

    def greet(k, whose):
        pl.semaphore_signal(barrier, inc=1, device_id=(whose(k),),
                            device_id_type=pl.DeviceIdType.MESH)

    def greet_mate(k, _):
        greet(k, mate)
        return 0

    def greet_twin(k, _):
        greet(k, twin)
        return 0

    lax.fori_loop(1, members, greet_mate, 0)
    lax.fori_loop(1, groups, greet_twin, 0)

    masks, slots = schedule(members)

    def piece(step):
        mask = 0
        for s, value in enumerate(masks):
            mask = value if s == 0 else jnp.where(step == s, value, mask)
        return partner_of(position, mask, bits)

    def loads(step):
        columns = pl.ds(pl.multiple_of(piece(step) * TILE, TILE), TILE)
        return (
            pltpu.make_async_copy(pix_ref.at[:, :, columns], pix.at[step], load_sem.at[0, step]),
            pltpu.make_async_copy(flag_ref.at[:, :, columns], flag.at[step], load_sem.at[1, step]),
        )

    def start_loads(step, _):
        for copy in loads(step):
            copy.start()
        return 0

    lax.fori_loop(0, members, start_loads, 0)

    def landing(sender):
        return out_ref.at[0, pl.ds(pl.multiple_of(sender * rows, rows), rows)]

    def delivery(step):
        return pltpu.make_async_remote_copy(
            src_ref=send.at[step],
            dst_ref=landing(position),
            send_sem=send_sem.at[step],
            recv_sem=recv_sem,
            device_id=(first + piece(step),),
            device_id_type=pl.DeviceIdType.MESH,
        )

    residue, spread, fix = lane_tables(bands)

    def work(step, totals, target):
        for copy in loads(step):
            copy.wait()
        totals = list(totals)
        for top in range(0, rows, SUBLANES):
            for left in range(0, TILE, LANES):
                spread_bands = []
                for b in range(bands):
                    x = pix[step, b, top:top + SUBLANES, left:left + LANES]
                    usable = flag[step, b, top:top + SUBLANES, left:left + LANES] == 1
                    filled = jnp.where(usable, x, 0.0)
                    low, high, count, total, squares = totals[b * STATS:(b + 1) * STATS]
                    totals[b * STATS:(b + 1) * STATS] = (
                        jnp.minimum(low, jnp.where(usable, x, largest_value)),
                        jnp.maximum(high, jnp.where(usable, x, -largest_value)),
                        count + jnp.where(usable, 1.0, 0.0),
                        total + filled,
                        squares + filled * filled,
                    )
                    spread_bands.append(permute(filled, spread[b]))
                for j in range(bands):
                    mixed = spread_bands[(bands - j) % bands]
                    for r in range(1, bands):
                        mixed = jnp.where(residue == r, spread_bands[(r - j) % bands], mixed)
                    if j:
                        mixed = permute(mixed, fix[j])
                    target(top, left * bands + j * LANES, mixed)
        return tuple(totals)

    def to_send(step):
        def put(top, left, value):
            send[step, top:top + SUBLANES, left:left + LANES] = value
        return put

    zero = jnp.zeros((SUBLANES, LANES), jnp.float32)
    totals = (zero + largest_value, zero - largest_value, zero, zero, zero) * bands
    totals = work(0, totals, to_send(0))
    pl.semaphore_wait(barrier, members - 1 + groups - 1)
    delivery(0).start()

    def work_and_send(step, totals):
        totals = work(step, totals, to_send(step))
        delivery(step).start()
        return totals

    def work_only(step, totals):
        return work(step, totals, to_send(step))

    totals = lax.fori_loop(1, early, work_and_send, totals)
    totals = lax.fori_loop(early, members - 1, work_only, totals)

    own = pl.multiple_of(position * rows, rows)

    def to_own(top, left, value):
        out_ref[0, pl.ds(own + top, SUBLANES), left:left + LANES] = value

    totals = work(members - 1, totals, to_own)

    lane = lax.broadcasted_iota(jnp.int32, (1, LANES), 1)
    line = jnp.zeros((1, LANES), jnp.float32)
    for b in range(bands):
        for s, reduce in enumerate((jnp.min, jnp.max, jnp.sum, jnp.sum, jnp.sum)):
            value = totals[b * STATS + s]
            value = reduce(reduce(value, axis=0, keepdims=True), axis=1, keepdims=True)
            line = jnp.where(lane == b * SLOT + s, value, line)
    row[0] = line
    rows_in[pl.ds(position, 1)] = line[None]

    def row_copy(k, stage, target, source):
        return pltpu.make_async_remote_copy(
            src_ref=row.at[stage],
            dst_ref=target,
            send_sem=row_send.at[stage],
            recv_sem=row_recv.at[stage],
            device_id=(source(k),),
            device_id_type=pl.DeviceIdType.MESH,
        )

    def start_row(k, _):
        row_copy(k, 0, rows_in.at[position], mate).start()
        return 0

    def start_group_row(k, _):
        row_copy(k, 1, stat_out.at[me // members], twin).start()
        return 0

    def merge_group():
        others = rows_in.at[pl.ds(0, members - 1)]
        pltpu.make_async_copy(others, others, row_recv.at[0]).wait()
        merged = merge_rows(rows_in[:, 0, :])
        row[1] = merged
        stat_out[pl.ds(me // members, 1)] = merged[None]
        lax.fori_loop(1, groups, start_group_row, 0)

    lax.fori_loop(1, members, start_row, 0)

    waited = set()
    for k, slot in enumerate(slots):
        if slot[0] < early:
            continue
        if k >= WINDOW:
            for step in slots[k - WINDOW]:
                delivery(step).wait_send()
                waited.add(step)
        for step in slot:
            delivery(step).start()
        if k == len(slots) // 2 + 1:
            merge_group()
    for step in range(members - 1):
        if step not in waited:
            delivery(step).wait_send()
    others = rows_in.at[pl.ds(0, members - 1)]
    pltpu.make_async_copy(others, others, row_send.at[0]).wait()
    if groups > 1:
        others = stat_out.at[pl.ds(0, groups - 1)]
        pltpu.make_async_copy(others, others, row_send.at[1]).wait()
        pltpu.make_async_copy(others, others, row_recv.at[1]).wait()
    arrived = out_ref.at[0, pl.ds(0, (members - 1) * rows)]
    pltpu.make_async_copy(arrived, arrived, recv_sem).wait()


def finish(bands, cell_total, chunks, tiles_ref, stats_ref, out_ref, header_ref, sem):
    height = tiles_ref.shape[1] // chunks
    copies = [
        pltpu.make_async_copy(
            tiles_ref.at[:, pl.ds(c * height, height)],
            out_ref.at[:, pl.ds(c * height, height)],
            sem.at[c],
        )
        for c in range(chunks)
    ]
    for copy in copies:
        copy.start()
    stats = stats_ref[:, 0, :]
    low = jnp.min(stats, axis=0, keepdims=True)
    high = jnp.max(stats, axis=0, keepdims=True)
    total = jnp.sum(stats, axis=0, keepdims=True)
    which = lax.broadcasted_iota(jnp.int32, (1, LANES), 1) % SLOT
    count = jnp.where(which == 2, total, 0.0)
    divisor = jnp.maximum(pltpu.roll(count, 1, 1) + pltpu.roll(count, 2, 1), 1.0)
    mean = total / divisor
    average = pltpu.roll(mean, 1, 1)
    deviation = jnp.sqrt(jnp.maximum(mean - average * average, 0.25))
    values = jnp.where(which == 3, mean, deviation)
    values = jnp.where(which == 2, total / cell_total, values)
    values = jnp.where(which == 1, high, values)
    values = jnp.where(which == 0, low, values)
    for b in range(bands):
        header_ref[b:b + 1, :] = values[:, b * SLOT:b * SLOT + STATS]
    for copy in copies:
        copy.wait()


def on_device(pixels, valid_flags):
    bands, rows, columns = pixels.shape
    n = lax.axis_size("dev")
    members = columns // TILE
    any_space = pl.BlockSpec(memory_space=pl.ANY)
    vmem_space = pl.BlockSpec(memory_space=pltpu.VMEM)
    tiles, stats = pl.pallas_call(
        functools.partial(exchange, n, members, EARLY),
        out_shape=(
            pltpu.VMEM((1, members * rows, TILE * bands), jnp.float32),
            pltpu.VMEM((n // members, 1, LANES), jnp.float32),
        ),
        in_specs=[any_space] * 2,
        out_specs=[vmem_space] * 2,
        scratch_shapes=[
            pltpu.VMEM((members, bands, rows, TILE), jnp.float32),
            pltpu.VMEM((members, bands, rows, TILE), jnp.int32),
            pltpu.VMEM((members - 1, rows, TILE * bands), jnp.float32),
            pltpu.VMEM((2, 1, LANES), jnp.float32),
            pltpu.VMEM((members, 1, LANES), jnp.float32),
            pltpu.SemaphoreType.DMA((2, members)),
            pltpu.SemaphoreType.DMA((members - 1,)),
            pltpu.SemaphoreType.DMA,
            pltpu.SemaphoreType.DMA((2,)),
            pltpu.SemaphoreType.DMA((2,)),
        ],
        compiler_params=pltpu.CompilerParams(collective_id=0, has_side_effects=True),
        name="exchange",
    )(pixels, valid_flags)
    chunks = 4
    tiles = pltpu.with_memory_space_constraint(tiles, pltpu.VMEM)
    stats = pltpu.with_memory_space_constraint(stats, pltpu.VMEM)
    out, header = pl.pallas_call(
        functools.partial(finish, bands, rows * columns * n, chunks),
        out_shape=(
            jax.ShapeDtypeStruct(tiles.shape, jnp.float32),
            jax.ShapeDtypeStruct((bands, STATS), jnp.float32),
        ),
        in_specs=[vmem_space] * 2,
        out_specs=[any_space, vmem_space],
        scratch_shapes=[pltpu.SemaphoreType.DMA((chunks,))],
        name="finish",
    )(tiles, stats)
    return out, header.T


def solution(mesh):
    in_specs = (P(None, "dev", None), P(None, "dev", None))
    out_specs = (P("dev", None, None), P())
    return jax.shard_map(
        on_device, mesh=mesh, in_specs=in_specs, out_specs=out_specs, check_vma=False
    )
```

profile of v0, /device:TPU:0, one launch (start us, length us, event | category | flops | bytes accessed | tf_op | source)
XLA Modules:
  0.0 33.7 jit_solution(14738120938618572792)
XLA Ops:
  0.6 31.1 %exchange.1 = (f32[1,256,2048]{2,1,0:T(8,128)S(1)}, f32[2,1,128]{2,1,0:T(1,128)S(1)}) custom-call(f32[4,16,8192]{2,1,0:T(8,128)} %pix_ref.1, s32[4,16,8192]{2,1,0:T(8,128)} %flag_ref.1), custom_call_target="tpu_custom_call" | custom-call | tf_op jit(solution)/shard_map/exchange/pallas_call | solution.py:294
  31.7 1.9 %finish.1 = (f32[1,256,2048]{2,1,0:T(8,128)}, f32[4,5]{1,0:T(4,128)}) custom-call(f32[1,256,2048]{2,1,0:T(8,128)S(1)} %get-tuple-element.6.tiles_ref, f32[2,1,128]{2,1,0:T(1,128)S(1)} %get-tuple-element.7.stats_ref), custom_call_target="tpu_custom_call" | custom-call | tf_op jit(solution)/shard_map/finish/pallas_call | solution.py:320
where the time goes:
time: 33.8 us; the launch traced here: 33.7 us
  Pallas kernels  33 us (98%)
  between operations  0.64 us (2%)
    pallas_call x1, Pallas kernels, on_device(): pl.pallas_call(functools.partial(exchange, n, members, EARLY), out_shape=...  31.1 us
    pallas_call x1, Pallas kernels, on_device(): pl.pallas_call(functools.partial(finish, bands, rows * columns * n, chunk...  1.92 us

commit v1 on v0

--- a/solution.py
+++ b/solution.py
@@ -253,7 +253,7 @@
     pltpu.make_async_copy(arrived, arrived, recv_sem).wait()
 
 
-def finish(bands, cell_total, chunks, tiles_ref, stats_ref, out_ref, header_ref, sem):
+def finish(bands, cell_total, chunks, tiles_ref, stats_ref, out_ref, header_ref, header, sem):
     height = tiles_ref.shape[1] // chunks
     copies = [
         pltpu.make_async_copy(
@@ -280,9 +280,12 @@
     values = jnp.where(which == 1, high, values)
     values = jnp.where(which == 0, low, values)
     for b in range(bands):
-        header_ref[b:b + 1, :] = values[:, b * SLOT:b * SLOT + STATS]
+        header[b:b + 1, :] = values[:, b * SLOT:b * SLOT + STATS]
+    header_copy = pltpu.make_async_copy(header, header_ref, sem.at[chunks])
+    header_copy.start()
     for copy in copies:
         copy.wait()
+    header_copy.wait()
 
 
 def on_device(pixels, valid_flags):
@@ -324,8 +327,11 @@
             jax.ShapeDtypeStruct((bands, STATS), jnp.float32),
         ),
         in_specs=[vmem_space] * 2,
-        out_specs=[any_space, vmem_space],
-        scratch_shapes=[pltpu.SemaphoreType.DMA((chunks,))],
+        out_specs=[any_space, any_space],
+        scratch_shapes=[
+            pltpu.VMEM((bands, STATS), jnp.float32),
+            pltpu.SemaphoreType.DMA((chunks + 1,)),
+        ],
         name="finish",
     )(tiles, stats)
     return out, header.T

time: 33.8 us -> 33.2 us (0.982)
  Pallas kernels: 33 us -> 32.5 us
    pallas_call x1, Pallas kernels: 1.92 us -> 1.36 us  [on_device(): pl.pallas_call(functools.partial(finish, bands, rows * columns * n, chunk...]
where the time goes in v1:
time: 33.2 us; the launch traced here: 33.1 us
  Pallas kernels  32.5 us (98%)
  between operations  0.64 us (2%)
    pallas_call x1, Pallas kernels, on_device(): pl.pallas_call(functools.partial(exchange, n, members, EARLY), out_shape=...  31.1 us
    pallas_call x1, Pallas kernels, on_device(): pl.pallas_call(functools.partial(finish, bands, rows * columns * n, chunk...  1.36 us

profile of v1, /device:TPU:0, one launch (start us, length us, event | category | flops | bytes accessed | tf_op | source)
XLA Modules:
  0.0 33.1 jit_solution(9177613680738728210)
XLA Ops:
  0.6 31.1 %exchange.1 = (f32[1,256,2048]{2,1,0:T(8,128)S(1)}, f32[2,1,128]{2,1,0:T(1,128)S(1)}) custom-call(f32[4,16,8192]{2,1,0:T(8,128)} %pix_ref.1, s32[4,16,8192]{2,1,0:T(8,128)} %flag_ref.1), custom_call_target="tpu_custom_call" | custom-call | tf_op jit(solution)/shard_map/exchange/pallas_call | solution.py:297
  31.7 1.4 %finish.1 = (f32[1,256,2048]{2,1,0:T(8,128)}, f32[4,5]{1,0:T(4,128)}) custom-call(f32[1,256,2048]{2,1,0:T(8,128)S(1)} %get-tuple-element.6.tiles_ref, f32[2,1,128]{2,1,0:T(1,128)S(1)} %get-tuple-element.7.stats_ref), custom_call_target="tpu_custom_call" | custom-call | tf_op jit(solution)/shard_map/finish/pallas_call | solution.py:323

commit v2 on v1

--- a/solution.py
+++ b/solution.py
@@ -13,32 +13,32 @@
 STATS = 5
 SLOT = 8
 WINDOW = 3
-EARLY = 2
+AHEAD = (0, 4)
 
 largest_value = 3e38
 
 
-def partner_of(position, mask, bits):
-    partner = position
-    for bit in range(bits):
-        own = position // (1 << bit) % 2
-        flip = mask // (1 << bit) % 2
-        partner = partner + flip * (1 - 2 * own) * (1 << bit)
-    return partner
-
-
 def schedule(members):
+    dims = members.bit_length() - 2
     whole = members // 2 - 1
-    pairs = sorted((min(high, whole - high, key=lambda h: (-h.bit_count(), h))
-                    for high in range(1, whole // 2 + 1)))
-    groups = [[(whole, 1)], [(whole, 0)]]
-    groups += [[(a, core), (whole - a, core)] for a in pairs for core in (0, 1)]
-    groups.append([(0, 1)])
+    near = [1 << dim for dim in range(dims)]
+    turns = {}
+    for dim in range(dims):
+        after = (dim + 1) % dims
+        turns.setdefault((1 << dim) + (1 << after), (dim, after))
+    relayed = [high for high in turns if high.bit_count() == 2 and high != whole]
+    paired = sorted((high for high in range(1, whole) if high > whole - high),
+                    key=lambda high: (-max(high.bit_count(), (whole - high).bit_count()), high))
+    left = [high for high in range(1, whole) if high.bit_count() > 1 and high not in relayed]
+    groups = [[(high, 0) for high in relayed], [(high, 0) for high in near], [(whole, 1)], [(whole, 0)]]
+    groups += [[(whole - high, 1), (high, 1)] for high in paired]
+    groups += [[(high, 0)] for high in left]
+    groups[4].append((0, 1))
     masks, slots = [], []
     for group in groups:
-        slots.append(range(len(masks), len(masks) + len(group)))
+        slots.append(list(range(len(masks), len(masks) + len(group))))
         masks += [high * 2 + core for high, core in group]
-    return masks + [0], slots
+    return masks + [0], slots, [turns[high] for high in relayed]
 
 
 def lane_tables(bands):
@@ -62,17 +62,25 @@
     return jnp.where(which == 0, low, jnp.where(which == 1, high, total))
 
 
-def exchange(n, members, early, pix_ref, flag_ref, out_ref, stat_out, pix, flag, send, row, rows_in,
-             load_sem, send_sem, recv_sem, row_send, row_recv):
+def exchange(n, members, pix_ref, flag_ref, out_ref, stat_out, pix, flag, send, row, rows_in,
+             relay, load_sem, send_sem, relay_send, relay_recv, recv_sem, row_send, row_recv, reach, cross):
     bands, rows, _ = pix_ref.shape
     bits = members.bit_length() - 1
+    groups = n // members
     me = lax.axis_index("dev")
     position = me % members
     first = me - position
-
-    barrier = pltpu.get_barrier_semaphore()
-
-    groups = n // members
+    keeper = members - 1
+    turns = [(1 - 2 * (position // (1 << bit) % 2)) * (1 << bit) for bit in range(bits)]
+    masks, slots, bends = schedule(members)
+    lead, soon = slots[0], slots[1]
+
+    def peer(mask):
+        where = position
+        for bit in range(bits):
+            if mask >> bit & 1:
+                where = where + turns[bit]
+        return where
 
     def mate(k):
         return first + (position + k) % members
@@ -80,63 +88,85 @@
     def twin(k):
         return (me + k * members) % n
 
-    def greet(k, whose):
-        pl.semaphore_signal(barrier, inc=1, device_id=(whose(k),),
+    def signal(semaphore, whom):
+        pl.semaphore_signal(semaphore, inc=1, device_id=(whom,),
                             device_id_type=pl.DeviceIdType.MESH)
 
-    def greet_mate(k, _):
-        greet(k, mate)
-        return 0
-
-    def greet_twin(k, _):
-        greet(k, twin)
-        return 0
-
-    lax.fori_loop(1, members, greet_mate, 0)
-    lax.fori_loop(1, groups, greet_twin, 0)
-
-    masks, slots = schedule(members)
-
-    def piece(step):
-        mask = 0
-        for s, value in enumerate(masks):
-            mask = value if s == 0 else jnp.where(step == s, value, mask)
-        return partner_of(position, mask, bits)
-
-    def loads(step):
-        columns = pl.ds(pl.multiple_of(piece(step) * TILE, TILE), TILE)
+    def loads(step, where):
+        columns = pl.ds(pl.multiple_of(where * TILE, TILE), TILE)
         return (
             pltpu.make_async_copy(pix_ref.at[:, :, columns], pix.at[step], load_sem.at[0, step]),
             pltpu.make_async_copy(flag_ref.at[:, :, columns], flag.at[step], load_sem.at[1, step]),
         )
 
-    def start_loads(step, _):
-        for copy in loads(step):
-            copy.start()
-        return 0
-
-    lax.fori_loop(0, members, start_loads, 0)
+    def start_loads(steps):
+        for step in steps:
+            for copy in loads(step, peer(masks[step])):
+                copy.start()
+
+    start_loads(lead)
+
+    def each(lo, hi, act):
+        def body(k, _):
+            act(k)
+            return 0
+
+        lax.fori_loop(lo, hi, body, 0)
+
+    barrier = pltpu.get_barrier_semaphore()
+    close = [1] + [(1 << bit) + core for bit in range(1, bits) for core in (0, 1)]
+    for mask in close:
+        signal(barrier, first + peer(mask))
+
+    @pl.when(position == keeper)
+    def _():
+        each(1, groups, lambda k: signal(barrier, twin(k)))
+
+    start_loads(range(len(lead), members))
+
+    def widen(level):
+        for bit in range(1, bits):
+            signal(reach.at[level], first + peer(1 << bit))
+
+    def copy_to(source, target, send_to, receive, mask):
+        return pltpu.make_async_remote_copy(
+            src_ref=source,
+            dst_ref=target,
+            send_sem=send_to,
+            recv_sem=receive,
+            device_id=(first + peer(mask),),
+            device_id_type=pl.DeviceIdType.MESH,
+        )
 
     def landing(sender):
         return out_ref.at[0, pl.ds(pl.multiple_of(sender * rows, rows), rows)]
 
+    def outbound(step, top=0, height=rows):
+        return copy_to(
+            send.at[step, pl.ds(top, height)], relay.at[step, pl.ds(top, height)],
+            send_sem.at[step], relay_recv.at[step], 2 << bends[step][0],
+        )
+
+    def forward(step):
+        start, after = bends[step]
+        return copy_to(
+            relay.at[step], landing(peer(2 << start)), relay_send.at[step], recv_sem, 2 << after
+        )
+
     def delivery(step):
-        return pltpu.make_async_remote_copy(
-            src_ref=send.at[step],
-            dst_ref=landing(position),
-            send_sem=send_sem.at[step],
-            recv_sem=recv_sem,
-            device_id=(first + piece(step),),
-            device_id_type=pl.DeviceIdType.MESH,
-        )
+        if step in lead:
+            return outbound(step)
+        return copy_to(send.at[step], landing(position), send_sem.at[step], recv_sem, masks[step])
 
     residue, spread, fix = lane_tables(bands)
 
-    def work(step, totals, target):
-        for copy in loads(step):
+    def wait_loads(step):
+        for copy in loads(step, 0):
             copy.wait()
+
+    def work(step, tops, totals, target):
         totals = list(totals)
-        for top in range(0, rows, SUBLANES):
+        for top in tops:
             for left in range(0, TILE, LANES):
                 spread_bands = []
                 for b in range(bands):
@@ -166,29 +196,51 @@
             send[step, top:top + SUBLANES, left:left + LANES] = value
         return put
 
+    tops = range(0, rows, SUBLANES)
+
+    def work_only(step, totals):
+        wait_loads(step)
+        return work(step, tops, totals, to_send(step))
+
     zero = jnp.zeros((SUBLANES, LANES), jnp.float32)
     totals = (zero + largest_value, zero - largest_value, zero, zero, zero) * bands
-    totals = work(0, totals, to_send(0))
-    pl.semaphore_wait(barrier, members - 1 + groups - 1)
-    delivery(0).start()
-
-    def work_and_send(step, totals):
-        totals = work(step, totals, to_send(step))
+    for top in tops:
+        for step in lead:
+            if top == 0:
+                wait_loads(step)
+            totals = work(step, (top,), totals, to_send(step))
+            if top == 0 and step == 0:
+                pl.semaphore_wait(barrier, len(close) + jnp.where(position == keeper, groups - 1, 0))
+                widen(0)
+            outbound(step, top, SUBLANES).start()
+    done = len(lead)
+    for step in soon:
+        totals = work_only(step, totals)
         delivery(step).start()
-        return totals
-
-    def work_only(step, totals):
-        return work(step, totals, to_send(step))
-
-    totals = lax.fori_loop(1, early, work_and_send, totals)
-    totals = lax.fori_loop(early, members - 1, work_only, totals)
+        done += 1
+
+    for level in range(bits - 2):
+        totals = lax.fori_loop(done, done + AHEAD[level], work_only, totals)
+        done += AHEAD[level]
+        pl.semaphore_wait(reach.at[level], bits - 1)
+        if level < bits - 3:
+            widen(level + 1)
+
+    @pl.when(position == keeper)
+    def _():
+        each(1, groups, lambda k: signal(cross, twin(k)))
+
+    for step in slots[2]:
+        delivery(step).start()
+    totals = lax.fori_loop(done, members - 1, work_only, totals)
 
     own = pl.multiple_of(position * rows, rows)
 
     def to_own(top, left, value):
         out_ref[0, pl.ds(own + top, SUBLANES), left:left + LANES] = value
 
-    totals = work(members - 1, totals, to_own)
+    wait_loads(members - 1)
+    totals = work(members - 1, tops, totals, to_own)
 
     lane = lax.broadcasted_iota(jnp.int32, (1, LANES), 1)
     line = jnp.zeros((1, LANES), jnp.float32)
@@ -198,57 +250,70 @@
             value = reduce(reduce(value, axis=0, keepdims=True), axis=1, keepdims=True)
             line = jnp.where(lane == b * SLOT + s, value, line)
     row[0] = line
-    rows_in[pl.ds(position, 1)] = line[None]
-
-    def row_copy(k, stage, target, source):
+    rows_in[keeper] = line
+
+    group = me // members
+
+    def row_copy(source, target, stage, whom):
         return pltpu.make_async_remote_copy(
-            src_ref=row.at[stage],
+            src_ref=source,
             dst_ref=target,
             send_sem=row_send.at[stage],
             recv_sem=row_recv.at[stage],
-            device_id=(source(k),),
+            device_id=(whom,),
             device_id_type=pl.DeviceIdType.MESH,
         )
 
-    def start_row(k, _):
-        row_copy(k, 0, rows_in.at[position], mate).start()
-        return 0
-
-    def start_group_row(k, _):
-        row_copy(k, 1, stat_out.at[me // members], twin).start()
-        return 0
-
-    def merge_group():
+    def to_keeper():
+        return row_copy(row.at[0], rows_in.at[position], 0, first + keeper)
+
+    def to_other(k):
+        return row_copy(row.at[1], stat_out.at[group], 1, (me + k) % n)
+
+    @pl.when(position != keeper)
+    def _():
+        to_keeper().start()
+
+    def share():
         others = rows_in.at[pl.ds(0, members - 1)]
         pltpu.make_async_copy(others, others, row_recv.at[0]).wait()
-        merged = merge_rows(rows_in[:, 0, :])
+        merged = merge_rows(rows_in[0:members, 0, :])
         row[1] = merged
-        stat_out[pl.ds(me // members, 1)] = merged[None]
-        lax.fori_loop(1, groups, start_group_row, 0)
-
-    lax.fori_loop(1, members, start_row, 0)
-
-    waited = set()
-    for k, slot in enumerate(slots):
-        if slot[0] < early:
-            continue
-        if k >= WINDOW:
-            for step in slots[k - WINDOW]:
-                delivery(step).wait_send()
-                waited.add(step)
-        for step in slot:
-            delivery(step).start()
-        if k == len(slots) // 2 + 1:
-            merge_group()
-    for step in range(members - 1):
-        if step not in waited:
-            delivery(step).wait_send()
-    others = rows_in.at[pl.ds(0, members - 1)]
-    pltpu.make_async_copy(others, others, row_send.at[0]).wait()
-    if groups > 1:
-        others = stat_out.at[pl.ds(0, groups - 1)]
-        pltpu.make_async_copy(others, others, row_send.at[1]).wait()
-        pltpu.make_async_copy(others, others, row_recv.at[1]).wait()
+        stat_out[pl.ds(group, 1)] = merged[None]
+        if groups > 1:
+            pl.semaphore_wait(cross, groups - 1)
+        each(1, n, lambda k: to_other(k).start())
+
+    sends = [[delivery(step) for step in slot] for slot in slots]
+    sends.insert(3, [forward(step) for step in lead])
+    started, waited = 3, 0
+    for k in range(started, len(sends)):
+        for copy in sends[k - WINDOW]:
+            copy.wait_send()
+        if k == 3:
+            for step in lead:
+                outbound(step).wait_recv()
+        for copy in sends[k]:
+            copy.start()
+        if k == len(sends) - 2:
+            pl.when(position == keeper)(share)
+    for k in range(len(sends) - WINDOW, len(sends)):
+        for copy in sends[k]:
+            copy.wait_send()
+
+    @pl.when(position == keeper)
+    def _():
+        sent = rows_in.at[pl.ds(0, n - 1)]
+        pltpu.make_async_copy(sent, sent, row_send.at[1]).wait()
+        if groups > 1:
+            others = stat_out.at[pl.ds(0, groups - 1)]
+            pltpu.make_async_copy(others, others, row_recv.at[1]).wait()
+
+    @pl.when(position != keeper)
+    def _():
+        to_keeper().wait_send()
+        pltpu.make_async_copy(stat_out, stat_out, row_recv.at[1]).wait()
+
     arrived = out_ref.at[0, pl.ds(0, (members - 1) * rows)]
     pltpu.make_async_copy(arrived, arrived, recv_sem).wait()
 
@@ -292,10 +357,11 @@
     bands, rows, columns = pixels.shape
     n = lax.axis_size("dev")
     members = columns // TILE
+    relays = len(schedule(members)[2])
     any_space = pl.BlockSpec(memory_space=pl.ANY)
     vmem_space = pl.BlockSpec(memory_space=pltpu.VMEM)
     tiles, stats = pl.pallas_call(
-        functools.partial(exchange, n, members, EARLY),
+        functools.partial(exchange, n, members),
         out_shape=(
             pltpu.VMEM((1, members * rows, TILE * bands), jnp.float32),
             pltpu.VMEM((n // members, 1, LANES), jnp.float32),
@@ -307,12 +373,17 @@
             pltpu.VMEM((members, bands, rows, TILE), jnp.int32),
             pltpu.VMEM((members - 1, rows, TILE * bands), jnp.float32),
             pltpu.VMEM((2, 1, LANES), jnp.float32),
-            pltpu.VMEM((members, 1, LANES), jnp.float32),
+            pltpu.VMEM((n, 1, LANES), jnp.float32),
+            pltpu.VMEM((relays, rows, TILE * bands), jnp.float32),
             pltpu.SemaphoreType.DMA((2, members)),
             pltpu.SemaphoreType.DMA((members - 1,)),
+            pltpu.SemaphoreType.DMA((relays,)),
+            pltpu.SemaphoreType.DMA((relays,)),
             pltpu.SemaphoreType.DMA,
             pltpu.SemaphoreType.DMA((2,)),
             pltpu.SemaphoreType.DMA((2,)),
+            pltpu.SemaphoreType.REGULAR((members.bit_length() - 3,)),
+            pltpu.SemaphoreType.REGULAR,
         ],
         compiler_params=pltpu.CompilerParams(collective_id=0, has_side_effects=True),
         name="exchange",

time: 33.2 us -> 31.6 us (0.952)
  Pallas kernels: 32.5 us -> 30.9 us
    pallas_call x1, Pallas kernels: 31.1 us -> 29.5 us  [on_device(): pl.pallas_call(functools.partial(exchange, n, members), out_shape=(pltpu....]
where the time goes in v2:
time: 31.6 us; the launch traced here: 31.5 us
  Pallas kernels  30.9 us (98%)
  between operations  0.64 us (2%)
    pallas_call x1, Pallas kernels, on_device(): pl.pallas_call(functools.partial(exchange, n, members), out_shape=(pltpu....  29.5 us
    pallas_call x1, Pallas kernels, on_device(): pl.pallas_call(functools.partial(finish, bands, rows * columns * n, chunk...  1.36 us

profile of v2, /device:TPU:0, one launch (start us, length us, event | category | flops | bytes accessed | tf_op | source)
XLA Modules:
  0.0 31.5 jit_solution(6153182960411915530)
XLA Ops:
  0.6 29.5 %exchange.1 = (f32[1,256,2048]{2,1,0:T(8,128)S(1)}, f32[2,1,128]{2,1,0:T(1,128)S(1)}) custom-call(f32[4,16,8192]{2,1,0:T(8,128)} %pix_ref.1, s32[4,16,8192]{2,1,0:T(8,128)} %flag_ref.1), custom_call_target="tpu_custom_call" | custom-call | tf_op jit(solution)/shard_map/exchange/pallas_call | solution.py:363
  30.1 1.4 %finish.1 = (f32[1,256,2048]{2,1,0:T(8,128)}, f32[4,5]{1,0:T(4,128)}) custom-call(f32[1,256,2048]{2,1,0:T(8,128)S(1)} %get-tuple-element.6.tiles_ref, f32[2,1,128]{2,1,0:T(1,128)S(1)} %get-tuple-element.7.stats_ref), custom_call_target="tpu_custom_call" | custom-call | tf_op jit(solution)/shard_map/finish/pallas_call | solution.py:394

commit v3 on v2

--- a/solution.py
+++ b/solution.py
@@ -13,7 +13,7 @@
 STATS = 5
 SLOT = 8
 WINDOW = 3
-AHEAD = (0, 4)
+AHEAD = 3
 
 largest_value = 3e38
 
@@ -82,6 +82,13 @@
                 where = where + turns[bit]
         return where
 
+    where = [peer(mask) for mask in masks]
+    late = where[slots[-1][0]] < 2
+    for step in slots[-1][1:]:
+        late = jnp.logical_or(late, where[step] < 2)
+    for a, b in zip(slots[-2], slots[-1]):
+        where[a], where[b] = jnp.where(late, where[b], where[a]), jnp.where(late, where[a], where[b])
+
     def mate(k):
         return first + (position + k) % members
 
@@ -101,7 +108,7 @@
 
     def start_loads(steps):
         for step in steps:
-            for copy in loads(step, peer(masks[step])):
+            for copy in loads(step, where[step]):
                 copy.start()
 
     start_loads(lead)
@@ -128,13 +135,13 @@
         for bit in range(1, bits):
             signal(reach.at[level], first + peer(1 << bit))
 
-    def copy_to(source, target, send_to, receive, mask):
+    def copy_to(source, target, send_to, receive, whom):
         return pltpu.make_async_remote_copy(
             src_ref=source,
             dst_ref=target,
             send_sem=send_to,
             recv_sem=receive,
-            device_id=(first + peer(mask),),
+            device_id=(first + whom,),
             device_id_type=pl.DeviceIdType.MESH,
         )
 
@@ -144,19 +151,23 @@
     def outbound(step, top=0, height=rows):
         return copy_to(
             send.at[step, pl.ds(top, height)], relay.at[step, pl.ds(top, height)],
-            send_sem.at[step], relay_recv.at[step], 2 << bends[step][0],
+            send_sem.at[step], relay_recv.at[step], peer(2 << bends[step][0]),
         )
 
     def forward(step):
         start, after = bends[step]
         return copy_to(
-            relay.at[step], landing(peer(2 << start)), relay_send.at[step], recv_sem, 2 << after
-        )
-
-    def delivery(step):
-        if step in lead:
-            return outbound(step)
-        return copy_to(send.at[step], landing(position), send_sem.at[step], recv_sem, masks[step])
+            relay.at[step], landing(peer(2 << start)), relay_send.at[step], recv_sem, peer(2 << after)
+        )
+
+    def delivery(step, top=0, height=rows):
+        start = pl.multiple_of(position * rows + top, SUBLANES)
+        return copy_to(
+            send.at[step, pl.ds(top, height)], out_ref.at[0, pl.ds(start, height)],
+            send_sem.at[step], recv_sem, where[step],
+        )
+
+    half = rows // 2 // SUBLANES * SUBLANES
 
     residue, spread, fix = lane_tables(bands)
 
@@ -204,27 +215,28 @@
 
     zero = jnp.zeros((SUBLANES, LANES), jnp.float32)
     totals = (zero + largest_value, zero - largest_value, zero, zero, zero) * bands
+    for step in lead:
+        wait_loads(step)
     for top in tops:
         for step in lead:
-            if top == 0:
-                wait_loads(step)
             totals = work(step, (top,), totals, to_send(step))
-            if top == 0 and step == 0:
-                pl.semaphore_wait(barrier, len(close) + jnp.where(position == keeper, groups - 1, 0))
-                widen(0)
+        if top == 0:
+            pl.semaphore_wait(barrier, len(close) + jnp.where(position == keeper, groups - 1, 0))
+            widen(0)
+        for step in lead:
             outbound(step, top, SUBLANES).start()
     done = len(lead)
-    for step in soon:
-        totals = work_only(step, totals)
-        delivery(step).start()
-        done += 1
-
     for level in range(bits - 2):
-        totals = lax.fori_loop(done, done + AHEAD[level], work_only, totals)
-        done += AHEAD[level]
         pl.semaphore_wait(reach.at[level], bits - 1)
         if level < bits - 3:
             widen(level + 1)
+        if level == 0:
+            for step in soon:
+                totals = work_only(step, totals)
+                delivery(step).start()
+                done += 1
+            totals = lax.fori_loop(done, done + AHEAD, work_only, totals)
+            done += AHEAD
 
     @pl.when(position == keeper)
     def _():
@@ -284,18 +296,23 @@
             pl.semaphore_wait(cross, groups - 1)
         each(1, n, lambda k: to_other(k).start())
 
-    sends = [[delivery(step) for step in slot] for slot in slots]
-    sends.insert(3, [forward(step) for step in lead])
-    started, waited = 3, 0
+    sends = [
+        [outbound(step) for step in lead],
+        [delivery(step) for step in soon],
+        [delivery(step) for step in slots[2]],
+        [forward(step) for step in lead],
+        *([delivery(step) for step in slot] for slot in slots[3:]),
+    ]
+    started = 3
     for k in range(started, len(sends)):
-        for copy in sends[k - WINDOW]:
+        for copy in sends[k - WINDOW] if k >= WINDOW else ():
             copy.wait_send()
         if k == 3:
             for step in lead:
                 outbound(step).wait_recv()
         for copy in sends[k]:
             copy.start()
-        if k == len(sends) - 2:
+        if k == 5:
             pl.when(position == keeper)(share)
     for k in range(len(sends) - WINDOW, len(sends)):
         for copy in sends[k]:

time: 31.6 us -> 31 us (0.981)
  the two profiles are of different devices: /device:TPU:0 before, /device:TPU:3 now
where the time goes in v3:
time: 31 us; the launch traced here: 30.9 us
  Pallas kernels  30.2 us (97%)
  between operations  0.64 us (2%)
    pallas_call x1, Pallas kernels, on_device(): pl.pallas_call(functools.partial(exchange, n, members), out_shape=(pltpu....  28.9 us
    pallas_call x1, Pallas kernels, on_device(): pl.pallas_call(functools.partial(finish, bands, rows * columns * n, chunk...  1.36 us

profile of v3, /device:TPU:3, one launch (start us, length us, event | category | flops | bytes accessed | tf_op | source)
XLA Modules:
  0.0 30.9 jit_solution(18356188294682643706)
XLA Ops:
  0.6 28.9 %exchange.1 = (f32[1,256,2048]{2,1,0:T(8,128)S(1)}, f32[2,1,128]{2,1,0:T(1,128)S(1)}) custom-call(f32[4,16,8192]{2,1,0:T(8,128)} %pix_ref.1, s32[4,16,8192]{2,1,0:T(8,128)} %flag_ref.1), custom_call_target="tpu_custom_call" | custom-call | tf_op jit(solution)/shard_map/exchange/pallas_call | solution.py:380
  29.5 1.4 %finish.1 = (f32[1,256,2048]{2,1,0:T(8,128)}, f32[4,5]{1,0:T(4,128)}) custom-call(f32[1,256,2048]{2,1,0:T(8,128)S(1)} %get-tuple-element.6.tiles_ref, f32[2,1,128]{2,1,0:T(1,128)S(1)} %get-tuple-element.7.stats_ref), custom_call_target="tpu_custom_call" | custom-call | tf_op jit(solution)/shard_map/finish/pallas_call | solution.py:411

commit v4 on v3

--- a/solution.py
+++ b/solution.py
@@ -70,7 +70,7 @@
     me = lax.axis_index("dev")
     position = me % members
     first = me - position
-    keeper = members - 1
+    keeper = 1
     turns = [(1 - 2 * (position // (1 << bit) % 2)) * (1 << bit) for bit in range(bits)]
     masks, slots, bends = schedule(members)
     lead, soon = slots[0], slots[1]
@@ -262,7 +262,7 @@
             value = reduce(reduce(value, axis=0, keepdims=True), axis=1, keepdims=True)
             line = jnp.where(lane == b * SLOT + s, value, line)
     row[0] = line
-    rows_in[keeper] = line
+    rows_in[members - 1] = line
 
     group = me // members
 
@@ -277,7 +277,7 @@
         )
 
     def to_keeper():
-        return row_copy(row.at[0], rows_in.at[position], 0, first + keeper)
+        return row_copy(row.at[0], rows_in.at[(position - keeper + members - 1) % members], 0, first + keeper)
 
     def to_other(k):
         return row_copy(row.at[1], stat_out.at[group], 1, (me + k) % n)

time: 31 us -> 30.3 us (0.977)
  the two profiles are of different devices: /device:TPU:3 before, /device:TPU:0 now
where the time goes in v4:
time: 30.3 us; the launch traced here: 30.1 us
  Pallas kernels  29.5 us (97%)
  between operations  0.64 us (2%)
    pallas_call x1, Pallas kernels, on_device(): pl.pallas_call(functools.partial(exchange, n, members), out_shape=(pltpu....  28.1 us
    pallas_call x1, Pallas kernels, on_device(): pl.pallas_call(functools.partial(finish, bands, rows * columns * n, chunk...  1.36 us

profile of v4, /device:TPU:0, one launch (start us, length us, event | category | flops | bytes accessed | tf_op | source)
XLA Modules:
  0.0 30.1 jit_solution(6144964754528278654)
XLA Ops:
  0.6 28.1 %exchange.1 = (f32[1,256,2048]{2,1,0:T(8,128)S(1)}, f32[2,1,128]{2,1,0:T(1,128)S(1)}) custom-call(f32[4,16,8192]{2,1,0:T(8,128)} %pix_ref.1, s32[4,16,8192]{2,1,0:T(8,128)} %flag_ref.1), custom_call_target="tpu_custom_call" | custom-call | tf_op jit(solution)/shard_map/exchange/pallas_call | solution.py:380
  28.7 1.4 %finish.1 = (f32[1,256,2048]{2,1,0:T(8,128)}, f32[4,5]{1,0:T(4,128)}) custom-call(f32[1,256,2048]{2,1,0:T(8,128)S(1)} %get-tuple-element.6.tiles_ref, f32[2,1,128]{2,1,0:T(1,128)S(1)} %get-tuple-element.7.stats_ref), custom_call_target="tpu_custom_call" | custom-call | tf_op jit(solution)/shard_map/finish/pallas_call | solution.py:411

commit v5 on v4

--- a/solution.py
+++ b/solution.py
@@ -12,7 +12,7 @@
 SUBLANES = 8
 STATS = 5
 SLOT = 8
-WINDOW = 3
+WINDOW = 5
 AHEAD = 3
 
 largest_value = 3e38
@@ -30,7 +30,7 @@
     paired = sorted((high for high in range(1, whole) if high > whole - high),
                     key=lambda high: (-max(high.bit_count(), (whole - high).bit_count()), high))
     left = [high for high in range(1, whole) if high.bit_count() > 1 and high not in relayed]
-    groups = [[(high, 0) for high in relayed], [(high, 0) for high in near], [(whole, 1)], [(whole, 0)]]
+    groups = [[(high, 0) for high in relayed], [(high, 0) for high in near], [(whole, 0)], [(whole, 1)]]
     groups += [[(whole - high, 1), (high, 1)] for high in paired]
     groups += [[(high, 0)] for high in left]
     groups[4].append((0, 1))
@@ -121,7 +121,7 @@
         lax.fori_loop(lo, hi, body, 0)
 
     barrier = pltpu.get_barrier_semaphore()
-    close = [1] + [(1 << bit) + core for bit in range(1, bits) for core in (0, 1)]
+    close = [1 << bit for bit in range(bits)]
     for mask in close:
         signal(barrier, first + peer(mask))
 
@@ -129,11 +129,10 @@
     def _():
         each(1, groups, lambda k: signal(barrier, twin(k)))
 
-    start_loads(range(len(lead), members))
 
     def widen(level):
-        for bit in range(1, bits):
-            signal(reach.at[level], first + peer(1 << bit))
+        for mask in close:
+            signal(reach.at[level], first + peer(mask))
 
     def copy_to(source, target, send_to, receive, whom):
         return pltpu.make_async_remote_copy(
@@ -225,16 +224,22 @@
             widen(0)
         for step in lead:
             outbound(step, top, SUBLANES).start()
+        if top == 0:
+            start_loads(range(len(lead), members))
     done = len(lead)
-    for level in range(bits - 2):
-        pl.semaphore_wait(reach.at[level], bits - 1)
-        if level < bits - 3:
+    for level in range(bits - 1):
+        pl.semaphore_wait(reach.at[level], bits)
+        if level < bits - 2:
             widen(level + 1)
         if level == 0:
             for step in soon:
                 totals = work_only(step, totals)
                 delivery(step).start()
                 done += 1
+        if level == bits - 3:
+            for step in slots[2]:
+                delivery(step).start()
+        if level < bits - 2:
             totals = lax.fori_loop(done, done + AHEAD, work_only, totals)
             done += AHEAD
 
@@ -242,8 +247,6 @@
     def _():
         each(1, groups, lambda k: signal(cross, twin(k)))
 
-    for step in slots[2]:
-        delivery(step).start()
     totals = lax.fori_loop(done, members - 1, work_only, totals)
 
     own = pl.multiple_of(position * rows, rows)
@@ -314,7 +317,7 @@
             copy.start()
         if k == 5:
             pl.when(position == keeper)(share)
-    for k in range(len(sends) - WINDOW, len(sends)):
+    for k in range(max(len(sends) - WINDOW, 0), len(sends)):
         for copy in sends[k]:
             copy.wait_send()
 
@@ -399,7 +402,7 @@
             pltpu.SemaphoreType.DMA,
             pltpu.SemaphoreType.DMA((2,)),
             pltpu.SemaphoreType.DMA((2,)),
-            pltpu.SemaphoreType.REGULAR((members.bit_length() - 3,)),
+            pltpu.SemaphoreType.REGULAR((members.bit_length() - 2,)),
             pltpu.SemaphoreType.REGULAR,
         ],
         compiler_params=pltpu.CompilerParams(collective_id=0, has_side_effects=True),

time: 30.3 us -> 30.1 us (level)
  Pallas kernels: 29.5 us -> 29 us
    pallas_call x1, Pallas kernels: 28.1 us -> 27.6 us  [on_device(): pl.pallas_call(functools.partial(exchange, n, members), out_shape=(pltpu....]
where the time goes in v5:
time: 30.1 us; the launch traced here: 29.6 us
  Pallas kernels  29 us (96%)
  between operations  0.64 us (2%)
    pallas_call x1, Pallas kernels, on_device(): pl.pallas_call(functools.partial(exchange, n, members), out_shape=(pltpu....  27.6 us
    pallas_call x1, Pallas kernels, on_device(): pl.pallas_call(functools.partial(finish, bands, rows * columns * n, chunk...  1.36 us

profile of v5, /device:TPU:0, one launch (start us, length us, event | category | flops | bytes accessed | tf_op | source)
XLA Modules:
  0.0 29.6 jit_solution(9120811456762192951)
XLA Ops:
  0.6 27.6 %exchange.1 = (f32[1,256,2048]{2,1,0:T(8,128)S(1)}, f32[2,1,128]{2,1,0:T(1,128)S(1)}) custom-call(f32[4,16,8192]{2,1,0:T(8,128)} %pix_ref.1, s32[4,16,8192]{2,1,0:T(8,128)} %flag_ref.1), custom_call_target="tpu_custom_call" | custom-call | tf_op jit(solution)/shard_map/exchange/pallas_call | solution.py:383
  28.3 1.4 %finish.1 = (f32[1,256,2048]{2,1,0:T(8,128)}, f32[4,5]{1,0:T(4,128)}) custom-call(f32[1,256,2048]{2,1,0:T(8,128)S(1)} %get-tuple-element.6.tiles_ref, f32[2,1,128]{2,1,0:T(1,128)S(1)} %get-tuple-element.7.stats_ref), custom_call_target="tpu_custom_call" | custom-call | tf_op jit(solution)/shard_map/finish/pallas_call | solution.py:414

commit v6 on v5

--- a/solution.py
+++ b/solution.py
@@ -88,6 +88,10 @@
         late = jnp.logical_or(late, where[step] < 2)
     for a, b in zip(slots[-2], slots[-1]):
         where[a], where[b] = jnp.where(late, where[b], where[a]), jnp.where(late, where[a], where[b])
+
+    last = position == members - 2
+    a, b = slots[-1][1], slots[-3][1]
+    where[a], where[b] = jnp.where(last, where[b], where[a]), jnp.where(last, where[a], where[b])
 
     def mate(k):
         return first + (position + k) % members
@@ -408,7 +412,7 @@
         compiler_params=pltpu.CompilerParams(collective_id=0, has_side_effects=True),
         name="exchange",
     )(pixels, valid_flags)
-    chunks = 4
+    chunks = 2
     tiles = pltpu.with_memory_space_constraint(tiles, pltpu.VMEM)
     stats = pltpu.with_memory_space_constraint(stats, pltpu.VMEM)
     out, header = pl.pallas_call(

time: 30.1 us -> 29.8 us (0.990)
  no operation moved by 1% of the time
where the time goes in v6:
time: 29.8 us; the launch traced here: 29.6 us
  Pallas kernels  29 us (97%)
  between operations  0.64 us (2%)
    pallas_call x1, Pallas kernels, on_device(): pl.pallas_call(functools.partial(exchange, n, members), out_shape=(pltpu....  27.6 us
    pallas_call x1, Pallas kernels, on_device(): pl.pallas_call(functools.partial(finish, bands, rows * columns * n, chunk...  1.35 us

profile of v6, /device:TPU:0, one launch (start us, length us, event | category | flops | bytes accessed | tf_op | source)
XLA Modules:
  0.0 29.6 jit_solution(2270763527813047593)
XLA Ops:
  0.6 27.6 %exchange.1 = (f32[1,256,2048]{2,1,0:T(8,128)S(1)}, f32[2,1,128]{2,1,0:T(1,128)S(1)}) custom-call(f32[4,16,8192]{2,1,0:T(8,128)} %pix_ref.1, s32[4,16,8192]{2,1,0:T(8,128)} %flag_ref.1), custom_call_target="tpu_custom_call" | custom-call | tf_op jit(solution)/shard_map/exchange/pallas_call | solution.py:387
  28.3 1.3 %finish.1 = (f32[1,256,2048]{2,1,0:T(8,128)}, f32[4,5]{1,0:T(4,128)}) custom-call(f32[1,256,2048]{2,1,0:T(8,128)S(1)} %get-tuple-element.6.tiles_ref, f32[2,1,128]{2,1,0:T(1,128)S(1)} %get-tuple-element.7.stats_ref), custom_call_target="tpu_custom_call" | custom-call | tf_op jit(solution)/shard_map/finish/pallas_call | solution.py:418

commit v7 on v6

--- a/solution.py
+++ b/solution.py
@@ -231,15 +231,14 @@
         if top == 0:
             start_loads(range(len(lead), members))
     done = len(lead)
+    for step in soon:
+        totals = work_only(step, totals)
+        delivery(step).start()
+        done += 1
     for level in range(bits - 1):
         pl.semaphore_wait(reach.at[level], bits)
         if level < bits - 2:
             widen(level + 1)
-        if level == 0:
-            for step in soon:
-                totals = work_only(step, totals)
-                delivery(step).start()
-                done += 1
         if level == bits - 3:
             for step in slots[2]:
                 delivery(step).start()

time: 29.8 us -> 29.8 us (level)
  no operation moved by 1% of the time
where the time goes in v7:
time: 29.8 us; the launch traced here: 29.6 us
  Pallas kernels  29 us (97%)
  between operations  0.64 us (2%)
    pallas_call x1, Pallas kernels, on_device(): pl.pallas_call(functools.partial(exchange, n, members), out_shape=(pltpu....  27.6 us
    pallas_call x1, Pallas kernels, on_device(): pl.pallas_call(functools.partial(finish, bands, rows * columns * n, chunk...  1.35 us

profile of v7, /device:TPU:0, one launch (start us, length us, event | category | flops | bytes accessed | tf_op | source)
XLA Modules:
  0.0 29.6 jit_solution(15550364004115820847)
XLA Ops:
  0.6 27.6 %exchange.1 = (f32[1,256,2048]{2,1,0:T(8,128)S(1)}, f32[2,1,128]{2,1,0:T(1,128)S(1)}) custom-call(f32[4,16,8192]{2,1,0:T(8,128)} %pix_ref.1, s32[4,16,8192]{2,1,0:T(8,128)} %flag_ref.1), custom_call_target="tpu_custom_call" | custom-call | tf_op jit(solution)/shard_map/exchange/pallas_call | solution.py:386
  28.3 1.3 %finish.1 = (f32[1,256,2048]{2,1,0:T(8,128)}, f32[4,5]{1,0:T(4,128)}) custom-call(f32[1,256,2048]{2,1,0:T(8,128)S(1)} %get-tuple-element.6.tiles_ref, f32[2,1,128]{2,1,0:T(1,128)S(1)} %get-tuple-element.7.stats_ref), custom_call_target="tpu_custom_call" | custom-call | tf_op jit(solution)/shard_map/finish/pallas_call | solution.py:417
